TPU v7x, 32 devices: a whole 2x2x4 slice. The times are simulated.
32 devices in a mesh: dp: 2 (over x), space: 4 (over y, core), mp: 4 (over z).
Axes of the slice: x: 2, y: 2, z: 4, core: 2. Of those that a mesh axis runs over, the one named last changes fastest.
Arguments:
- teacher_tokens: bfloat16 [16, 4, 16, 16, 1408], P('dp', 'space'), parts along dimension 0, may hold values from -16 to 16
- student_tokens: bfloat16 [16, 4, 16, 16, 1280], P('dp', 'space'), parts along dimension 0, may hold values from -16 to 16
- teacher_head: bfloat16 [2816, 1000], P(('dp', 'space'), 'mp'), parts along dimension 0, may hold values from -1 to 1
- student_head: bfloat16 [2560, 1000], P(('dp', 'space'), 'mp'), parts along dimension 0, may hold values from -1 to 1
- valid: int32 [16, 4, 16, 16], P('dp', 'space'), parts along dimension 0, may hold values from 0 to 1, as said below
Outputs:
- patch_kl: float32 [16, 4, 16, 16], P('dp', 'space'), parts along dimension 0
- image_loss: float32 [16], P('dp'), parts along dimension 0
There are 2 independent parts, one for each index of `dp`. A program takes and returns all parts, laid end to end along the dimension named above; each array names one. Nothing has to cross between parts.
Inputs may be any that keep to these rules, and one draw needn't show every extreme that they name: An image may have no valid patch.
All inputs are finite; a program needn't handle non-finite values.
Results may differ from a plain program's by a relative error of at most 0.0003.
Values may be sent and summed in bfloat16 or wider, within the bound.
A program may use at most 64 MiB of HBM per device.

v0:
```python
import functools
import math

import jax
import jax.numpy as jnp
from jax import lax
from jax.experimental import pallas as pl
from jax.experimental.pallas import tpu as pltpu
from jax.sharding import PartitionSpec as P

MESH = pl.DeviceIdType.MESH
F32 = jnp.float32
BF16 = jnp.bfloat16


def kernel(
    edge, mp, parts_w,
    tt_hbm, ts_hbm, wt_hbm, ws_hbm, valid_hbm,
    kl_hbm, loss_hbm,
    tt, ts, wt, ws, hi, lo, sl, smat, rowbuf, colbuf, corbuf, corh, stats, gath, tot, gtot, wide,
    valid_ref, kl_ref, loss_ref, log_student,
    loc_sem, wsend, wrecv, hsend, hrecv, ssend, srecv, tsend, trecv,
):
    t = lax.axis_index("space")
    m = lax.axis_index("mp")
    row, col = t // 2, t % 2
    across = 1 - col + 2 * row
    below = col + 2 * (1 - row)
    diag = 3 - t
    images = tt.shape[0]
    area = edge * edge

    barrier = pltpu.get_barrier_semaphore()
    for peer in (across, below, diag):
        pl.semaphore_signal(barrier, inc=1, device_id={"space": peer}, device_id_type=MESH)
    for d in range(1, mp):
        pl.semaphore_signal(barrier, inc=1, device_id={"mp": lax.rem(m + d, mp)}, device_id_type=MESH)

    local = []
    for k, (src, w) in enumerate(((wt_hbm, wt), (ws_hbm, ws))):
        n = src.shape[0]
        dst = w.at[pl.ds(pl.multiple_of(t * n, 16), n)]
        local.append(pltpu.make_async_copy(src, dst, loc_sem.at[k]))
    local.append(pltpu.make_async_copy(tt_hbm, tt, loc_sem.at[2]))
    local.append(pltpu.make_async_copy(ts_hbm, ts, loc_sem.at[3]))
    local.append(pltpu.make_async_copy(valid_hbm, valid_ref, loc_sem.at[4]))
    for c in local:
        c.start()

    local[0].wait()
    pl.semaphore_wait(barrier, 3 + mp - 1)

    def piece(w, owner, chunk):
        n = w.shape[0] // 4
        size = n // parts_w
        return w.at[pl.ds(pl.multiple_of(owner * n + chunk * size, 16), size)]

    def move(w, k, kind, owner, chunk, peer):
        i = (k * 3 + kind) * parts_w + chunk
        ref = piece(w, owner, chunk)
        return pltpu.make_async_remote_copy(
            src_ref=ref, dst_ref=ref, send_sem=wsend.at[i], recv_sem=wrecv.at[i],
            device_id={"space": peer}, device_id_type=MESH,
        )

    moves = {}
    for k, w in enumerate((wt, ws)):
        for chunk in range(parts_w):
            moves[k, 0, chunk] = move(w, k, 0, t, chunk, below)
            moves[k, 1, chunk] = move(w, k, 1, t, chunk, across)
            moves[k, 2, chunk] = move(w, k, 2, below, chunk, across)
    for k in range(2):
        if k == 1:
            local[1].wait()
        for chunk in range(parts_w):
            moves[k, 0, chunk].start()
            moves[k, 1, chunk].start()

    p_y = lax.broadcasted_iota(jnp.int32, (edge, edge, area + 2 * edge), 0).reshape(area, area + 2 * edge)
    p_x = lax.broadcasted_iota(jnp.int32, (edge, edge, area + 2 * edge), 1).reshape(area, area + 2 * edge)
    q = lax.broadcasted_iota(jnp.int32, (area, area + 2 * edge), 1)
    e_y = (edge - 1) * (1 - row)
    e_x = (edge - 1) * (1 - col)
    h_y = edge * (1 - row) - row
    h_x = edge * (1 - col) - col
    in_row = (q >= area) & (q < area + edge)
    in_col = q >= area + edge
    q_y = jnp.where(in_row, h_y, jnp.where(in_col, q - area - edge, q // edge))
    q_x = jnp.where(in_row, q - area, jnp.where(in_col, h_x, q % edge))
    near = (jnp.abs(p_y - q_y) <= 1) & (jnp.abs(p_x - q_x) <= 1)
    smat[...] = jnp.where(near, 1.0, 0.0).astype(BF16)

    local[4].wait()
    for r in range(edge):
        wide[:, r * edge : (r + 1) * edge] = valid_ref[:, r, :].astype(F32)

    def arrive(k, w):
        for chunk in range(parts_w):
            move(w, k, 0, below, chunk, below).wait_recv()
            moves[k, 2, chunk].start()
        for chunk in range(parts_w):
            move(w, k, 1, across, chunk, across).wait_recv()
            move(w, k, 2, diag, chunk, across).wait_recv()

    arrive(0, wt)
    local[2].wait()
    edge_tokens = tt[:, pl.ds(pl.multiple_of(e_y * edge, 16), edge), :].reshape(images * edge, tt.shape[-1])
    edge_row = jnp.dot(edge_tokens, wt[...], preferred_element_type=F32).reshape(images, edge, -1)
    rowbuf[...] = edge_row.astype(BF16)
    corbuf[...] = jnp.where(col == 0, edge_row[:, edge - 1, :], edge_row[:, 0, :])
    row_move = pltpu.make_async_remote_copy(
        src_ref=rowbuf, dst_ref=hi.at[:, pl.ds(area, edge), :], send_sem=hsend.at[0], recv_sem=hrecv.at[0],
        device_id={"space": below}, device_id_type=MESH,
    )
    cor_move = pltpu.make_async_remote_copy(
        src_ref=corbuf, dst_ref=corh, send_sem=hsend.at[1], recv_sem=hrecv.at[1],
        device_id={"space": diag}, device_id_type=MESH,
    )
    row_move.start()
    cor_move.start()

    def teacher_dot(i, carry):
        x = jnp.dot(tt[i], wt[...], preferred_element_type=F32)
        top = x.astype(BF16)
        hi[i, pl.ds(0, area), :] = top
        lo[i] = (x - top.astype(F32)).astype(BF16)
        x3 = x.reshape(edge, edge, x.shape[-1])
        side_x = jnp.where(col == 0, x3[:, edge - 1, :], x3[:, 0, :])
        colbuf[i] = side_x.astype(BF16)
        return carry

    lax.fori_loop(0, images, teacher_dot, 0, unroll=8)
    col_move = pltpu.make_async_remote_copy(
        src_ref=colbuf, dst_ref=hi.at[:, pl.ds(area + edge, edge), :], send_sem=hsend.at[2], recv_sem=hrecv.at[2],
        device_id={"space": across}, device_id_type=MESH,
    )
    col_move.start()

    arrive(1, ws)
    local[3].wait()

    def student_dot(i, carry):
        student = jnp.dot(ts[i], ws[...], preferred_element_type=F32)
        sl[i] = student
        top_s = jnp.max(student, axis=-1, keepdims=True)
        sum_s = jnp.sum(jnp.exp(student - top_s), axis=-1, keepdims=True)
        log_student[i] = top_s + jnp.log(sum_s)
        return carry

    lax.fori_loop(0, images, student_dot, 0, unroll=8)

    y = lax.broadcasted_iota(jnp.int32, (edge, edge, 1), 0).reshape(area, 1)
    x = lax.broadcasted_iota(jnp.int32, (edge, edge, 1), 1).reshape(area, 1)
    last = 2 * edge - 1
    g_y, g_x = y + row * edge, x + col * edge
    line_y = 1.0 + jnp.where(g_y > 0, 1.0, 0.0) + jnp.where(g_y < last, 1.0, 0.0)
    line_x = 1.0 + jnp.where(g_x > 0, 1.0, 0.0) + jnp.where(g_x < last, 1.0, 0.0)
    inverse = 1.0 / (line_y * line_x)
    at_corner = (y == e_y) & (x == e_x)

    row_move.wait_recv()
    cor_move.wait_recv()
    col_move.wait_recv()

    lane = lax.broadcasted_iota(jnp.int32, (area, 128), 1)

    def image_stats(i, carry):
        total = jnp.dot(smat[...], hi[i], preferred_element_type=F32)
        total += jnp.dot(smat[:, :area], lo[i], preferred_element_type=F32)
        total += jnp.where(at_corner, corh[pl.ds(i, 1), :], 0.0)
        smooth = total * inverse
        student = sl[i]
        top_t = jnp.max(smooth, axis=-1, keepdims=True)
        expo = jnp.exp(smooth - top_t)
        sum_t = jnp.sum(expo, axis=-1, keepdims=True)
        mean = jnp.sum(expo * (smooth - student), axis=-1, keepdims=True) / sum_t
        log_t = top_t + jnp.log(sum_t)
        log_s = log_student[i]
        packed = jnp.where(lane == 0, log_t, jnp.where(lane == 1, mean, log_s))
        turned = packed.T
        for k in range(3):
            stats[k, pl.ds(i, 1), :] = turned[k : k + 1, :]
        return carry

    lax.fori_loop(0, images, image_stats, 0, unroll=4)

    sends = []
    for d in range(1, mp):
        c = pltpu.make_async_remote_copy(
            src_ref=stats, dst_ref=gath.at[d - 1], send_sem=ssend.at[d - 1], recv_sem=srecv.at[d - 1],
            device_id={"mp": lax.rem(m + d, mp)}, device_id_type=MESH,
        )
        c.start()
        sends.append(c)
    for c in sends:
        c.wait_recv()
    logs_t = [stats[0]] + [gath[d, 0] for d in range(mp - 1)]
    means = [stats[1]] + [gath[d, 1] for d in range(mp - 1)]
    logs_s = [stats[2]] + [gath[d, 2] for d in range(mp - 1)]
    top_t = functools.reduce(jnp.maximum, logs_t)
    top_s = functools.reduce(jnp.maximum, logs_s)
    shares = [jnp.exp(v - top_t) for v in logs_t]
    sum_t = sum(shares)
    sum_s = sum(jnp.exp(v - top_s) for v in logs_s)
    weighted = sum(a * b for a, b in zip(shares, means))
    kl = weighted / sum_t - top_t - jnp.log(sum_t) + top_s + jnp.log(sum_s)
    weights = wide[...]
    total = jnp.sum(kl * weights, axis=-1, keepdims=True)
    number = jnp.sum(weights, axis=-1, keepdims=True)
    lanes = lax.broadcasted_iota(jnp.int32, (images, 128), 1)
    tot[...] = jnp.where(lanes == 0, total, number)
    shares_out = []
    for k, peer in enumerate((across, below, diag)):
        c = pltpu.make_async_remote_copy(
            src_ref=tot, dst_ref=gtot.at[k], send_sem=tsend.at[k], recv_sem=trecv.at[k],
            device_id={"space": peer}, device_id_type=MESH,
        )
        c.start()
        shares_out.append(c)
    for r in range(edge):
        kl_ref[:, r, :] = kl[:, r * edge : (r + 1) * edge]
    kl_out = pltpu.make_async_copy(kl_ref, kl_hbm, loc_sem.at[5])
    kl_out.start()
    for c in sends + [row_move, cor_move, col_move] + list(moves.values()):
        c.wait_send()
    for c in shares_out:
        c.wait_recv()
    everything = tot[...] + gtot[0] + gtot[1] + gtot[2]
    loss = everything[:, 0:1] / jnp.maximum(everything[:, 1:2], 1.0)
    loss_ref[...] = jnp.broadcast_to(loss, (images, 128)).T[0:1, :]
    loss_out = pltpu.make_async_copy(loss_ref, loss_hbm, loc_sem.at[6])
    loss_out.start()
    for c in shares_out:
        c.wait_send()
    kl_out.wait()
    loss_out.wait()


def finish(kl_in, loss_in, kl_out, loss_out):
    kl_out[...] = kl_in[...]
    loss_out[...] = loss_in[...]


def fused(teacher_tokens, student_tokens, teacher_head, student_head, valid):
    images, _, edge, _, width = teacher_tokens.shape
    swidth = student_tokens.shape[-1]
    area = edge * edge
    classes = teacher_head.shape[1]
    mp = lax.axis_size("mp")
    parts_w = 2 if teacher_head.shape[0] % 32 == 0 and student_head.shape[0] % 32 == 0 else 1
    anywhere = pl.BlockSpec(memory_space=pl.ANY)
    dma = pltpu.SemaphoreType.DMA
    kl, loss = pl.pallas_call(
        functools.partial(kernel, edge, mp, parts_w),
        out_shape=(
            jax.ShapeDtypeStruct((images, edge, edge), F32),
            jax.ShapeDtypeStruct((1, images), F32),
        ),
        in_specs=[anywhere] * 5,
        out_specs=(anywhere, anywhere),
        scratch_shapes=[
            pltpu.VMEM((images, area, width), BF16),
            pltpu.VMEM((images, area, swidth), BF16),
            pltpu.VMEM((width, classes), BF16),
            pltpu.VMEM((swidth, classes), BF16),
            pltpu.VMEM((images, area + 2 * edge, classes), BF16),
            pltpu.VMEM((images, area, classes), BF16),
            pltpu.VMEM((images, area, classes), F32),
            pltpu.VMEM((area, area + 2 * edge), BF16),
            pltpu.VMEM((images, edge, classes), BF16),
            pltpu.VMEM((images, edge, classes), BF16),
            pltpu.VMEM((images, classes), F32),
            pltpu.VMEM((images, classes), F32),
            pltpu.VMEM((3, images, area), F32),
            pltpu.VMEM((mp - 1, 3, images, area), F32),
            pltpu.VMEM((images, 128), F32),
            pltpu.VMEM((3, images, 128), F32),
            pltpu.VMEM((images, area), F32),
            pltpu.VMEM((images, edge, edge), jnp.int32),
            pltpu.VMEM((images, edge, edge), F32),
            pltpu.VMEM((1, images), F32),
            pltpu.VMEM((images, area, 1), F32),
            dma((7,)),
            dma((6 * parts_w,)),
            dma((6 * parts_w,)),
            dma((3,)),
            dma((3,)),
            dma((mp - 1,)),
            dma((mp - 1,)),
            dma((3,)),
            dma((3,)),
        ],
        compiler_params=pltpu.CompilerParams(collective_id=0, has_side_effects=True),
    )(
        teacher_tokens.reshape(images, area, width),
        student_tokens.reshape(images, area, swidth),
        teacher_head,
        student_head,
        valid.reshape(images, edge, edge),
    )
    whole = pl.BlockSpec(memory_space=pltpu.VMEM)
    kl, loss = pl.pallas_call(
        finish,
        out_shape=(jax.ShapeDtypeStruct(kl.shape, F32), jax.ShapeDtypeStruct(loss.shape, F32)),
        in_specs=[whole, whole],
        out_specs=(whole, whole),
    )(kl, loss)
    return kl.reshape(images, 1, edge, edge), loss.reshape(images)


def shifted(block, axis, distance):
    devices = range(lax.axis_size(axis))
    route = [(i - distance, i) for i in devices if i - distance in devices]
    return lax.ppermute(block, axis, route)


def logit_move(values, offset):
    return shifted(values, "space", offset)


def extend(values, mover, side, column):
    left = mover(values[:, :, -1:, :], 1)
    left = jnp.where(column > 0, left, jnp.zeros_like(left))
    right = mover(values[:, :, :1, :], -1)
    right = jnp.where(column < side - 1, right, jnp.zeros_like(right))
    wide = jnp.concatenate([left, values, right], axis=2)
    upper = mover(wide[:, -1:, :, :], side)
    lower = mover(wide[:, :1, :, :], -side)
    return jnp.concatenate([upper, wide, lower], axis=1)


def body(teacher_tokens, student_tokens, teacher_head, student_head, valid):
    side = math.isqrt(lax.axis_size("space"))
    tile_index = lax.axis_index("space")
    tile_row = tile_index // side
    tile_column = tile_index % side
    teacher_tile = teacher_tokens[:, 0]
    student_tile = student_tokens[:, 0]
    images, edge = (teacher_tile.shape[0], teacher_tile.shape[1])
    classes_here = teacher_head.shape[1]
    source_flat = teacher_tile.reshape(-1, teacher_tile.shape[-1])
    student_flat = student_tile.reshape(-1, student_tile.shape[-1])
    teacher_logits = jnp.dot(
        source_flat,
        lax.all_gather(teacher_head, "space", axis=0, tiled=True),
        preferred_element_type=jnp.float32,
    )
    student_logits = jnp.dot(
        student_flat,
        lax.all_gather(student_head, "space", axis=0, tiled=True),
        preferred_element_type=jnp.float32,
    )
    teacher_wide = extend(
        teacher_logits.reshape(images, edge, edge, classes_here), logit_move, side, tile_column
    )
    extent = side * edge
    total = jnp.zeros((images, edge, edge, classes_here), jnp.float32)
    for shift_y in range(3):
        for shift_x in range(3):
            total = total + teacher_wide[:, shift_y : shift_y + edge, shift_x : shift_x + edge, :]
    places_y = tile_row * edge + jnp.arange(edge)
    places_x = tile_column * edge + jnp.arange(edge)
    line_y = 1.0 + (places_y > 0).astype(jnp.float32) + (places_y < extent - 1).astype(jnp.float32)
    line_x = 1.0 + (places_x > 0).astype(jnp.float32) + (places_x < extent - 1).astype(jnp.float32)
    counts = line_y[:, None] * line_x[None, :]
    smoothed = total / counts[None, :, :, None]
    student = student_logits.reshape(images, edge, edge, classes_here)
    top_t, top_s = lax.pmax((jnp.max(smoothed, axis=-1), jnp.max(student, axis=-1)), "mp")
    expo_t = jnp.exp(smoothed - top_t[..., None])
    sum_t, weighted, sum_s = lax.psum(
        (
            jnp.sum(expo_t, axis=-1),
            jnp.sum(expo_t * (smoothed - student), axis=-1),
            jnp.sum(jnp.exp(student - top_s[..., None]), axis=-1),
        ),
        "mp",
    )
    divergence = weighted / sum_t - top_t - jnp.log(sum_t) + top_s + jnp.log(sum_s)
    weights = valid[:, 0].astype(jnp.float32)
    totals, numbers = lax.psum(
        (jnp.sum(divergence * weights, axis=(1, 2)), jnp.sum(weights, axis=(1, 2))), "space"
    )
    image_loss = totals / jnp.maximum(numbers, 1.0)
    return (divergence[:, None], image_loss)


def chosen(teacher_tokens, student_tokens, teacher_head, student_head, valid):
    operands = (teacher_tokens, student_tokens, teacher_head, student_head, valid)
    aligned = (
        lax.axis_size("space") == 4
        and lax.axis_size("mp") > 1
        and teacher_tokens.shape[2] % 16 == 0
        and teacher_head.shape[0] % 16 == 0
        and student_head.shape[0] % 16 == 0
        and teacher_tokens.shape[0] % 8 == 0
    )
    return fused(*operands) if aligned else body(*operands)


def solution(mesh):
    in_specs = (
        P("dp", "space", None, None, None),
        P("dp", "space", None, None, None),
        P(("dp", "space"), "mp"),
        P(("dp", "space"), "mp"),
        P("dp", "space", None, None),
    )
    out_specs = (P("dp", "space", None, None), P("dp"))
    return jax.shard_map(chosen, mesh=mesh, in_specs=in_specs, out_specs=out_specs, check_vma=False)
```

profile of v0, /device:TPU:0, one launch (start us, length us, event | category | flops | bytes accessed | tf_op | source)
XLA Modules:
  0.0 29.1 jit_solution(1839787332695358148)
XLA Ops:
  0.6 27.0 %shard_map.68 = (f32[8,16,16]{2,1,0:T(8,128)}, f32[1,8]{1,0:T(1,128)}) custom-call(bf16[8,256,1408]{2,1,0:T(8,128)(2,1)} %bitcast.7, bf16[8,256,1280]{2,1,0:T(8,128)(2,1)} %bitcast.8, bf16[352,250]{1,0:T(8,128)(2,1)} %wt_hbm.1, bf16[320,250]{1,0:T(8,128)(2,1)} %ws_hbm.1, s32[8,16,16]{2,1,0:T(8,128)} %bitcast.9), custom_call_target="tpu_custom_call" | custom-call | tf_op jit(solution)/shard_map/pallas_call | solution.py:253
  27.6 1.5 %shard_map.69 = (f32[8,16,16]{2,1,0:T(8,128)}, f32[1,8]{1,0:T(1,128)}) custom-call(f32[8,16,16]{2,1,0:T(8,128)} %get-tuple-element.6.kl_in, f32[1,8]{1,0:T(1,128)} %get-tuple-element.7.loss_in), custom_call_target="tpu_custom_call" | custom-call | tf_op jit(solution)/shard_map/pallas_call | solution.py:302
where the time goes:
time: 29.3 us; the launch traced here: 29.1 us
  Pallas kernels  28.5 us (97%)
  between operations  0.64 us (2%)
    pallas_call x1, Pallas kernels, fused(): pl.pallas_call(functools.partial(kernel, edge, mp, parts_w), out_shape=(j...  27 us
    pallas_call x1, Pallas kernels, fused(): pl.pallas_call(finish, out_shape=(jax.ShapeDtypeStruct(kl.shape, F32), ja...  1.48 us

commit v1 on v0

--- a/solution.py
+++ b/solution.py
@@ -19,7 +19,7 @@
     kl_hbm, loss_hbm,
     tt, ts, wt, ws, hi, lo, sl, smat, rowbuf, colbuf, corbuf, corh, stats, gath, tot, gtot, wide,
     valid_ref, kl_ref, loss_ref, log_student,
-    loc_sem, wsend, wrecv, hsend, hrecv, ssend, srecv, tsend, trecv,
+    loc_sem, wsend, wrecv, hsend, hrecv, ssend, srecv, tsend, trecv, known,
 ):
     t = lax.axis_index("space")
     m = lax.axis_index("mp")
@@ -33,8 +33,15 @@
     barrier = pltpu.get_barrier_semaphore()
     for peer in (across, below, diag):
         pl.semaphore_signal(barrier, inc=1, device_id={"space": peer}, device_id_type=MESH)
-    for d in range(1, mp):
-        pl.semaphore_signal(barrier, inc=1, device_id={"mp": lax.rem(m + d, mp)}, device_id_type=MESH)
+    has_left, has_right = m > 0, m < mp - 1
+
+    @pl.when(has_left)
+    def _():
+        pl.semaphore_signal(barrier, inc=1, device_id={"mp": m - 1}, device_id_type=MESH)
+
+    @pl.when(has_right)
+    def _():
+        pl.semaphore_signal(barrier, inc=1, device_id={"mp": m + 1}, device_id_type=MESH)
 
     local = []
     for k, (src, w) in enumerate(((wt_hbm, wt), (ws_hbm, ws))):
@@ -48,7 +55,7 @@
         c.start()
 
     local[0].wait()
-    pl.semaphore_wait(barrier, 3 + mp - 1)
+    pl.semaphore_wait(barrier, 3 + has_left.astype(jnp.int32) + has_right.astype(jnp.int32))
 
     def piece(w, owner, chunk):
         n = w.shape[0] // 4
@@ -75,6 +82,20 @@
         for chunk in range(parts_w):
             moves[k, 0, chunk].start()
             moves[k, 1, chunk].start()
+
+    def present(k, side, step):
+        @pl.when((m + step >= 0) & (m + step < mp) & (m - k * step >= 0) & (m - k * step < mp))
+        def _():
+            pl.semaphore_signal(known.at[side, k - 1], inc=1, device_id={"mp": m + step}, device_id_type=MESH)
+
+    def heard(k, side, step):
+        @pl.when((m - step >= 0) & (m - step < mp) & (m - (k + 1) * step >= 0) & (m - (k + 1) * step < mp))
+        def _():
+            pl.semaphore_wait(known.at[side, k - 1], 1)
+
+    if mp > 2:
+        for side, step in enumerate((1, -1)):
+            present(1, side, step)
 
     p_y = lax.broadcasted_iota(jnp.int32, (edge, edge, area + 2 * edge), 0).reshape(area, area + 2 * edge)
     p_x = lax.broadcasted_iota(jnp.int32, (edge, edge, area + 2 * edge), 1).reshape(area, area + 2 * edge)
@@ -138,6 +159,11 @@
 
     arrive(1, ws)
     local[3].wait()
+    for k in range(1, mp - 1):
+        for side, step in enumerate((1, -1)):
+            heard(k, side, step)
+            if k < mp - 2:
+                present(k + 1, side, step)
 
     def student_dot(i, carry):
         student = jnp.dot(ts[i], ws[...], preferred_element_type=F32)
@@ -289,6 +315,7 @@
             dma((mp - 1,)),
             dma((3,)),
             dma((3,)),
+            pltpu.SemaphoreType.REGULAR((2, max(mp - 2, 1))),
         ],
         compiler_params=pltpu.CompilerParams(collective_id=0, has_side_effects=True),
     )(

time: 29.3 us -> 29.8 us (1.017)
  Pallas kernels: 28.5 us -> 29 us
    pallas_call x1, Pallas kernels: 27 us -> 27.5 us  [fused(): pl.pallas_call(functools.partial(kernel, edge, mp, parts_w), out_shape=(j...]
where the time goes in v1:
time: 29.8 us; the launch traced here: 29.7 us
  Pallas kernels  29 us (97%)
  between operations  0.64 us (2%)
    pallas_call x1, Pallas kernels, fused(): pl.pallas_call(functools.partial(kernel, edge, mp, parts_w), out_shape=(j...  27.5 us
    pallas_call x1, Pallas kernels, fused(): pl.pallas_call(finish, out_shape=(jax.ShapeDtypeStruct(kl.shape, F32), ja...  1.48 us

profile of v1, /device:TPU:0, one launch (start us, length us, event | category | flops | bytes accessed | tf_op | source)
XLA Modules:
  0.0 29.7 jit_solution(15113950080750070802)
XLA Ops:
  0.6 27.5 %shard_map.68 = (f32[8,16,16]{2,1,0:T(8,128)}, f32[1,8]{1,0:T(1,128)}) custom-call(bf16[8,256,1408]{2,1,0:T(8,128)(2,1)} %bitcast.7, bf16[8,256,1280]{2,1,0:T(8,128)(2,1)} %bitcast.8, bf16[352,250]{1,0:T(8,128)(2,1)} %wt_hbm.1, bf16[320,250]{1,0:T(8,128)(2,1)} %ws_hbm.1, s32[8,16,16]{2,1,0:T(8,128)} %bitcast.9), custom_call_target="tpu_custom_call" | custom-call | tf_op jit(solution)/shard_map/pallas_call | solution.py:279
  28.2 1.5 %shard_map.69 = (f32[8,16,16]{2,1,0:T(8,128)}, f32[1,8]{1,0:T(1,128)}) custom-call(f32[8,16,16]{2,1,0:T(8,128)} %get-tuple-element.6.kl_in, f32[1,8]{1,0:T(1,128)} %get-tuple-element.7.loss_in), custom_call_target="tpu_custom_call" | custom-call | tf_op jit(solution)/shard_map/pallas_call | solution.py:329

commit v2 on v0

v2 whole, which is shorter than its diff:
```python
import functools
import math

import jax
import jax.numpy as jnp
from jax import lax
from jax.experimental import pallas as pl
from jax.experimental.pallas import tpu as pltpu
from jax.sharding import PartitionSpec as P

MESH = pl.DeviceIdType.MESH
F32 = jnp.float32
BF16 = jnp.bfloat16


def kernel(
    edge, mp,
    tt_hbm, ts_hbm, wt_hbm, ws_hbm, valid_hbm,
    kl_ref, loss_ref,
    tt, ts, wt, ws, tt_w, ts_w, pre, sl, ex, ec, smat, scol, srow, slift, spick, hal, row_out, col_hl, tok_out, tok_x,
    stat_s, stat_t, gath_s, gath_t, tot, gtot, wide, kl_buf,
    valid_ref,
    loc_sem, wsend, wrecv, hsend, hrecv, ssend, srecv, tsend, trecv,
):
    t = lax.axis_index("space")
    m = lax.axis_index("mp")
    row, col = t // 2, t % 2
    across = 1 - col + 2 * row
    below = col + 2 * (1 - row)
    diag = 3 - t
    images = tt.shape[0]
    area = edge * edge
    groups = stat_t.shape[0]
    per = images // groups
    n_edge = images * edge

    barrier = pltpu.get_barrier_semaphore()
    for peer in (across, below, diag):
        pl.semaphore_signal(barrier, inc=1, device_id={"space": peer}, device_id_type=MESH)
    for d in range(1, mp):
        pl.semaphore_signal(barrier, inc=1, device_id={"mp": lax.rem(m + d, mp)}, device_id_type=MESH)

    local = []
    for k, (src, w) in enumerate(((wt_hbm, wt), (ws_hbm, ws))):
        n = src.shape[0]
        dst = w.at[pl.ds(pl.multiple_of(t * n, 16), n)]
        local.append(pltpu.make_async_copy(src, dst, loc_sem.at[k]))
    local.append(pltpu.make_async_copy(tt_hbm, tt, loc_sem.at[2]))
    local.append(pltpu.make_async_copy(ts_hbm, ts, loc_sem.at[3]))
    local.append(pltpu.make_async_copy(valid_hbm, valid_ref, loc_sem.at[4]))
    for c in local:
        c.start()

    local[0].wait()
    pl.semaphore_wait(barrier, 3 + mp - 1)

    def piece(w, owner, chunk):
        n = w.shape[0] // 4
        large = split(n)
        side = lax.rem(owner, 2)
        if chunk == 0:
            start, size = owner * n + side * (n - large), large
        else:
            start, size = owner * n + (1 - side) * large, n - large
        return w.at[pl.ds(pl.multiple_of(start, 16), size)]

    def move(w, k, kind, owner, chunk, peer):
        i = (k * 3 + kind) * 2 + chunk
        ref = piece(w, owner, chunk)
        return pltpu.make_async_remote_copy(
            src_ref=ref, dst_ref=ref, send_sem=wsend.at[i], recv_sem=wrecv.at[i],
            device_id={"space": peer}, device_id_type=MESH,
        )

    moves = {}
    for k, w in enumerate((wt, ws)):
        for chunk in range(2):
            moves[k, 0, chunk] = move(w, k, 0, t, chunk, below)
            moves[k, 1, chunk] = move(w, k, 1, t, chunk, across)
            moves[k, 2, chunk] = move(w, k, 2, below, chunk, across)
    for k in range(2):
        if k == 1:
            local[1].wait()
        for chunk in range(2):
            if k == 0:
                moves[k, 0, chunk].start()
            moves[k, 1, chunk].start()

    e_y = (edge - 1) * (1 - row)
    e_x = (edge - 1) * (1 - col)

    def one_hot(where):
        return jnp.where(where, 1.0, 0.0).astype(BF16)

    def iota(shape, axis):
        return lax.broadcasted_iota(jnp.int32, shape, axis)

    half = area // 2
    una, aff = pl.multiple_of(row * half, 128), pl.multiple_of((1 - row) * half, 128)
    q, p = iota((area, area), 0), iota((area, area), 1)
    smat[...] = one_hot((jnp.abs(p // edge - q // edge) <= 1) & (jnp.abs(p % edge - q % edge) <= 1))
    h, p = iota((n_edge, area), 0), iota((n_edge, area), 1)
    from_col = (p % edge == e_x) & (jnp.abs(p // edge - h % edge) <= 1)
    h2, p2 = iota((n_edge, half), 0), iota((n_edge, half), 1) + aff
    from_row = (p2 // edge == e_y) & (p2 % edge == h2 % edge)
    for i in range(images):
        scol[i, 0:n_edge, :] = one_hot(from_col & (h // edge == i))
        scol[i, n_edge:, :] = scol[i, 0:n_edge, :]
        srow[i] = one_hot(from_row & (h2 // edge == i))
    a, b = iota((n_edge, n_edge), 0), iota((n_edge, n_edge), 1)
    slift[0:n_edge, :] = one_hot((a // edge == b // edge) & (jnp.abs(a - b) <= 1))
    slift[n_edge:, :] = one_hot((a == b // edge * edge + e_y) & (b % edge == e_x))
    a, b = iota((edge, area), 0), iota((edge, area), 1)
    spick[...] = one_hot(b == a * edge + e_x)
    p = iota((1, area), 1)
    last = 2 * edge - 1
    g_y, g_x = p // edge + row * edge, p % edge + col * edge
    line_y = 1.0 + jnp.where(g_y > 0, 1.0, 0.0) + jnp.where(g_y < last, 1.0, 0.0)
    line_x = 1.0 + jnp.where(g_x > 0, 1.0, 0.0) + jnp.where(g_x < last, 1.0, 0.0)
    inverse = 1.0 / (line_y * line_x)

    def nn(x, y):
        return jnp.dot(x, y, preferred_element_type=F32)

    local[2].wait()
    for i in range(images):
        tok_out[i * edge : (i + 1) * edge, :] = nn(spick[...], tt[i]).astype(BF16)
    tok_move = pltpu.make_async_remote_copy(
        src_ref=tok_out, dst_ref=tok_x.at[pl.ds(n_edge, n_edge)], send_sem=hsend.at[1], recv_sem=hrecv.at[1],
        device_id={"space": across}, device_id_type=MESH,
    )
    tok_move.start()
    tok_x[0:n_edge, :] = tt[:, pl.ds(pl.multiple_of(e_y * edge, 16), edge), :].reshape(n_edge, tt.shape[-1])

    local[4].wait()
    for r in range(edge):
        wide[:, r * edge : (r + 1) * edge] = valid_ref[:, r, :].astype(F32)

    def turn(w, w_t, start, size):
        for j in range(0, size, 128):
            at = pl.multiple_of(start + j, 128)
            w_t[:, pl.ds(at, 128)] = w[pl.ds(at, 128), :].T

    def times(w_t, tokens, start, size):
        at = pl.ds(pl.multiple_of(start, 128), size)
        return lax.dot_general(
            w_t[:, at], tokens[:, at], (((1,), (1,)), ((), ())), preferred_element_type=F32
        )

    def own(k, w):
        for chunk in range(2):
            move(w, k, 1, across, chunk, across).wait_recv()

    def arrive(k, w, chunk):
        move(w, k, 0, below, chunk, below).wait_recv()
        moves[k, 2, chunk].start()

    def arrive_far(k, w, chunk):
        move(w, k, 2, diag, chunk, across).wait_recv()

    def each(f):
        lax.fori_loop(0, images, f, 0, unroll=images)

    class Parts:
        def __init__(self, k):
            large = split(k // 4)
            near = k // 256 * 128
            first, second, far = middle(k)
            self.near = near
            self.outer, self.inner = first, second - first
            self.near_at = row * (k - near)
            self.one_at = (1 - row) * (k - far)
            self.two_at = row * second + (1 - row) * (k - first)
            self.mid_at = row * first + (1 - row) * (k - second)

    of_t, of_s = Parts(tt.shape[-1]), Parts(ts.shape[-1])
    own(0, wt)
    turn(wt, tt_w, of_t.near_at, of_t.near)

    def teacher_near(i, carry):
        pre[i] = times(tt_w, tt.at[i], of_t.near_at, of_t.near)
        return carry

    each(teacher_near)
    own(1, ws)
    turn(ws, ts_w, of_s.near_at, of_s.near)
    local[3].wait()

    def student_near(i, carry):
        sl[i] = times(ts_w, ts.at[i], of_s.near_at, of_s.near)
        return carry

    each(student_near)
    for chunk in range(2):
        moves[0, 0, chunk].wait_send()
    for chunk in range(2):
        moves[1, 0, chunk].start()
    tok_move.wait_recv()
    ec[...] = times(tt_w, tok_x, of_t.near_at, of_t.near)

    arrive(0, wt, 0)
    arrive(0, wt, 1)
    arrive_far(0, wt, 0)
    turn(wt, tt_w, of_t.one_at, of_t.outer)
    turn(wt, tt_w, of_t.two_at, of_t.outer)
    ec[...] += times(tt_w, tok_x, of_t.one_at, of_t.outer) + times(tt_w, tok_x, of_t.two_at, of_t.outer)

    def teacher_outer(i, carry):
        pre[i] += times(tt_w, tt.at[i], of_t.one_at, of_t.outer) + times(tt_w, tt.at[i], of_t.two_at, of_t.outer)
        return carry

    each(teacher_outer)
    arrive_far(0, wt, 1)
    turn(wt, tt_w, of_t.mid_at, of_t.inner)

    def two(x):
        top = x.astype(BF16)
        return top, (x - top.astype(F32)).astype(BF16)

    e_hi, e_lo = two(ec[...] + times(tt_w, tok_x, of_t.mid_at, of_t.inner))
    row_out[...] = (nn(e_hi, slift[...]) + nn(e_lo, slift[...])).astype(BF16)
    row_move = pltpu.make_async_remote_copy(
        src_ref=row_out, dst_ref=hal, send_sem=hsend.at[0], recv_sem=hrecv.at[0],
        device_id={"space": below}, device_id_type=MESH,
    )
    col_hl[:, 0:n_edge] = e_hi[:, n_edge:]
    col_hl[:, n_edge:] = e_lo[:, n_edge:]

    def teacher_inner(i, carry):
        top, rest = two(pre[i] + times(tt_w, tt.at[i], of_t.mid_at, of_t.inner))
        pre[i] = (nn(top, smat[...]) + nn(rest, smat[...]) + nn(col_hl[...], scol[i])) * inverse
        return carry

    each(teacher_inner)

    for chunk in range(2):
        moves[1, 0, chunk].wait_send()
    row_move.start()

    def teacher_half(i, carry):
        top = jnp.max(pre[i, :, pl.ds(una, half)], axis=0, keepdims=True)
        expo = jnp.exp(pre[i, :, pl.ds(una, half)] - top)
        ex[i] = expo
        total = jnp.sum(expo, axis=0, keepdims=True)
        stat_t[i // per, pl.ds(i % per, 1), pl.ds(una, half)] = top + jnp.log(total)
        stat_t[i // per, pl.ds(per + i % per, 1), pl.ds(una, half)] = 1.0 / total
        return carry

    for i in range(images):
        teacher_half(i, 0)

    arrive(1, ws, 0)
    arrive(1, ws, 1)
    arrive_far(1, ws, 0)
    turn(ws, ts_w, of_s.one_at, of_s.outer)
    turn(ws, ts_w, of_s.two_at, of_s.outer)

    def student_outer(i, carry):
        sl[i] += times(ts_w, ts.at[i], of_s.one_at, of_s.outer) + times(ts_w, ts.at[i], of_s.two_at, of_s.outer)
        return carry

    each(student_outer)
    arrive_far(1, ws, 1)
    turn(ws, ts_w, of_s.mid_at, of_s.inner)

    def student_stats(i, carry):
        student = sl[i] + times(ts_w, ts.at[i], of_s.mid_at, of_s.inner)
        sl[i] = student
        top = jnp.max(student, axis=0, keepdims=True)
        total = jnp.sum(jnp.exp(sl[i] - top), axis=0, keepdims=True)
        stat_s[pl.ds(i, 1), :] = top + jnp.log(total)
        gap = pre[i, :, pl.ds(una, half)] - sl[i, :, pl.ds(una, half)]
        at = (i // per, pl.ds(per + i % per, 1), pl.ds(una, half))
        stat_t[at] = jnp.sum(ex[i] * gap, axis=0, keepdims=True) * stat_t[at]
        return carry

    for i in range(images):
        student_stats(i, 0)

    sends, arriving = [], {}

    def share(src, dst, k):
        for j in range(mp - 1):
            up, down = mp - 1 - j, j
            peer = jnp.where(2 * m < mp, up - (up <= m).astype(jnp.int32), down + (down >= m).astype(jnp.int32))
            slot = lax.rem(peer - m + mp, mp) - 1
            c = pltpu.make_async_remote_copy(
                src_ref=src, dst_ref=dst(slot), send_sem=ssend.at[k, j], recv_sem=srecv.at[k, slot],
                device_id={"mp": peer}, device_id_type=MESH,
            )
            c.start()
            sends.append(c)
        for d in range(mp - 1):
            arriving[k, d] = pltpu.make_async_remote_copy(
                src_ref=src, dst_ref=dst(d), send_sem=ssend.at[k, d], recv_sem=srecv.at[k, d],
                device_id={"mp": lax.rem(m + d + 1, mp)}, device_id_type=MESH,
            )

    share(stat_s, lambda d: gath_s.at[d], groups)

    row_move.wait_recv()
    scale = jnp.where(row == 0, inverse[:, half:], inverse[:, 0:half])
    for g in range(groups):
        for j in range(per):
            i = g * per + j
            smooth = pre[i, :, pl.ds(aff, half)] + nn(hal[...], srow[i]) * scale
            top = jnp.max(smooth, axis=0, keepdims=True)
            expo = jnp.exp(smooth - top)
            total = jnp.sum(expo, axis=0, keepdims=True)
            gap = smooth - sl[i, :, pl.ds(aff, half)]
            mean = jnp.sum(expo * gap, axis=0, keepdims=True) / total
            stat_t[g, pl.ds(j, 1), pl.ds(aff, half)] = top + jnp.log(total)
            stat_t[g, pl.ds(per + j, 1), pl.ds(aff, half)] = mean
        share(stat_t.at[g], lambda d, g=g: gath_t.at[d, g], g)

    def wait_shared(k):
        for d in range(mp - 1):
            arriving[k, d].wait_recv()

    wait_shared(groups)
    for g in range(groups):
        wait_shared(g)
        mine = [stat_t[g]] + [gath_t[d, g] for d in range(mp - 1)]
        logs_t = [v[0:per] for v in mine]
        means = [v[per : 2 * per] for v in mine]
        rows = slice(g * per, (g + 1) * per)
        logs_s = [stat_s[rows, :]] + [gath_s[d, rows, :] for d in range(mp - 1)]
        top_t = functools.reduce(jnp.maximum, logs_t)
        top_s = functools.reduce(jnp.maximum, logs_s)
        shares = [jnp.exp(v - top_t) for v in logs_t]
        sum_t = sum(shares)
        sum_s = sum(jnp.exp(v - top_s) for v in logs_s)
        weighted = sum(a * b for a, b in zip(shares, means))
        kl_buf[rows, :] = weighted / sum_t - top_t - jnp.log(sum_t) + top_s + jnp.log(sum_s)
    kl = kl_buf[...]
    weights = wide[...]
    total = jnp.sum(kl * weights, axis=-1, keepdims=True)
    number = jnp.sum(weights, axis=-1, keepdims=True)
    lanes = iota((images, 128), 1)
    tot[...] = jnp.where(lanes == 0, total, number)
    shares_out = []
    for k, peer in enumerate((across, below, diag)):
        c = pltpu.make_async_remote_copy(
            src_ref=tot, dst_ref=gtot.at[k], send_sem=tsend.at[k], recv_sem=trecv.at[k],
            device_id={"space": peer}, device_id_type=MESH,
        )
        c.start()
        shares_out.append(c)
    for r in range(edge):
        kl_ref[:, r, :] = kl[:, r * edge : (r + 1) * edge]
    for c in sends + [row_move, tok_move] + [c for key, c in moves.items() if key[1] != 0]:
        c.wait_send()
    for c in shares_out:
        c.wait_recv()
    everything = tot[...] + gtot[0] + gtot[1] + gtot[2]
    loss = everything[:, 0:1] / jnp.maximum(everything[:, 1:2], 1.0)
    diagonal = jnp.where(lanes == iota((images, 128), 0), loss, 0.0)
    loss_ref[...] = jnp.sum(diagonal, axis=0, keepdims=True)[:, 0:images]
    for c in shares_out:
        c.wait_send()


def middle(k):
    large = split(k // 4)
    first = large // 128 * 128
    second = -(-(k // 2 - large) // 128) * 128
    return first, second, k - k // 256 * 128


def split(rows):
    large = rows // 128 * 128
    return large if large < rows else rows - 128


def finish(kl_in, loss_in, kl_out, loss_out, sem):
    copies = [pltpu.make_async_copy(kl_in, kl_out, sem.at[0]), pltpu.make_async_copy(loss_in, loss_out, sem.at[1])]
    for c in copies:
        c.start()
    for c in copies:
        c.wait()


def fused(teacher_tokens, student_tokens, teacher_head, student_head, valid):
    images, _, edge, _, width = teacher_tokens.shape
    swidth = student_tokens.shape[-1]
    area = edge * edge
    n_edge = images * edge
    classes = teacher_head.shape[1]
    mp = lax.axis_size("mp")
    groups = 1
    anywhere = pl.BlockSpec(memory_space=pl.ANY)
    whole = pl.BlockSpec(memory_space=pltpu.VMEM)
    dma = pltpu.SemaphoreType.DMA
    kl, loss = pl.pallas_call(
        functools.partial(kernel, edge, mp),
        out_shape=(
            pltpu.VMEM((images, edge, edge), F32),
            pltpu.VMEM((1, images), F32),
        ),
        in_specs=[anywhere] * 5,
        out_specs=(whole, whole),
        scratch_shapes=[
            pltpu.VMEM((images, area, width), BF16),
            pltpu.VMEM((images, area, swidth), BF16),
            pltpu.VMEM((width, classes), BF16),
            pltpu.VMEM((swidth, classes), BF16),
            pltpu.VMEM((classes, width), BF16),
            pltpu.VMEM((classes, swidth), BF16),
            pltpu.VMEM((images, classes, area), F32),
            pltpu.VMEM((images, classes, area), F32),
            pltpu.VMEM((images, classes, area // 2), F32),
            pltpu.VMEM((classes, 2 * n_edge), F32),
            pltpu.VMEM((area, area), BF16),
            pltpu.VMEM((images, 2 * n_edge, area), BF16),
            pltpu.VMEM((images, n_edge, area // 2), BF16),
            pltpu.VMEM((2 * n_edge, n_edge), BF16),
            pltpu.VMEM((edge, area), BF16),
            pltpu.VMEM((classes, n_edge), BF16),
            pltpu.VMEM((classes, n_edge), BF16),
            pltpu.VMEM((classes, 2 * n_edge), BF16),
            pltpu.VMEM((n_edge, width), BF16),
            pltpu.VMEM((2 * n_edge, width), BF16),
            pltpu.VMEM((images, area), F32),
            pltpu.VMEM((groups, 2 * images // groups, area), F32),
            pltpu.VMEM((mp - 1, images, area), F32),
            pltpu.VMEM((mp - 1, groups, 2 * images // groups, area), F32),
            pltpu.VMEM((images, 128), F32),
            pltpu.VMEM((3, images, 128), F32),
            pltpu.VMEM((images, area), F32),
            pltpu.VMEM((images, area), F32),
            pltpu.VMEM((images, edge, edge), jnp.int32),
            dma((5,)),
            dma((12,)),
            dma((12,)),
            dma((2,)),
            dma((2,)),
            dma((groups + 1, mp - 1)),
            dma((groups + 1, mp - 1)),
            dma((3,)),
            dma((3,)),
        ],
        compiler_params=pltpu.CompilerParams(collective_id=0, has_side_effects=True),
    )(
        teacher_tokens.reshape(images, area, width),
        student_tokens.reshape(images, area, swidth),
        teacher_head,
        student_head,
        valid.reshape(images, edge, edge),
    )
    kl, loss = pl.pallas_call(
        finish,
        out_shape=(jax.ShapeDtypeStruct(kl.shape, F32), jax.ShapeDtypeStruct(loss.shape, F32)),
        in_specs=[whole, whole],
        out_specs=(anywhere, anywhere),
        scratch_shapes=[dma((2,))],
    )(pltpu.with_memory_space_constraint(kl, pltpu.VMEM), pltpu.with_memory_space_constraint(loss, pltpu.VMEM))
    return kl.reshape(images, 1, edge, edge), loss.reshape(images)


def shifted(block, axis, distance):
    devices = range(lax.axis_size(axis))
    route = [(i - distance, i) for i in devices if i - distance in devices]
    return lax.ppermute(block, axis, route)


def logit_move(values, offset):
    return shifted(values, "space", offset)


def extend(values, mover, side, column):
    left = mover(values[:, :, -1:, :], 1)
    left = jnp.where(column > 0, left, jnp.zeros_like(left))
    right = mover(values[:, :, :1, :], -1)
    right = jnp.where(column < side - 1, right, jnp.zeros_like(right))
    wide = jnp.concatenate([left, values, right], axis=2)
    upper = mover(wide[:, -1:, :, :], side)
    lower = mover(wide[:, :1, :, :], -side)
    return jnp.concatenate([upper, wide, lower], axis=1)


def body(teacher_tokens, student_tokens, teacher_head, student_head, valid):
    side = math.isqrt(lax.axis_size("space"))
    tile_index = lax.axis_index("space")
    tile_row = tile_index // side
    tile_column = tile_index % side
    teacher_tile = teacher_tokens[:, 0]
    student_tile = student_tokens[:, 0]
    images, edge = (teacher_tile.shape[0], teacher_tile.shape[1])
    classes_here = teacher_head.shape[1]
    source_flat = teacher_tile.reshape(-1, teacher_tile.shape[-1])
    student_flat = student_tile.reshape(-1, student_tile.shape[-1])
    teacher_logits = jnp.dot(
        source_flat,
        lax.all_gather(teacher_head, "space", axis=0, tiled=True),
        preferred_element_type=jnp.float32,
    )
    student_logits = jnp.dot(
        student_flat,
        lax.all_gather(student_head, "space", axis=0, tiled=True),
        preferred_element_type=jnp.float32,
    )
    teacher_wide = extend(
        teacher_logits.reshape(images, edge, edge, classes_here), logit_move, side, tile_column
    )
    extent = side * edge
    total = jnp.zeros((images, edge, edge, classes_here), jnp.float32)
    for shift_y in range(3):
        for shift_x in range(3):
            total = total + teacher_wide[:, shift_y : shift_y + edge, shift_x : shift_x + edge, :]
    places_y = tile_row * edge + jnp.arange(edge)
    places_x = tile_column * edge + jnp.arange(edge)
    line_y = 1.0 + (places_y > 0).astype(jnp.float32) + (places_y < extent - 1).astype(jnp.float32)
    line_x = 1.0 + (places_x > 0).astype(jnp.float32) + (places_x < extent - 1).astype(jnp.float32)
    counts = line_y[:, None] * line_x[None, :]
    smoothed = total / counts[None, :, :, None]
    student = student_logits.reshape(images, edge, edge, classes_here)
    top_t, top_s = lax.pmax((jnp.max(smoothed, axis=-1), jnp.max(student, axis=-1)), "mp")
    expo_t = jnp.exp(smoothed - top_t[..., None])
    sum_t, weighted, sum_s = lax.psum(
        (
            jnp.sum(expo_t, axis=-1),
            jnp.sum(expo_t * (smoothed - student), axis=-1),
            jnp.sum(jnp.exp(student - top_s[..., None]), axis=-1),
        ),
        "mp",
    )
    divergence = weighted / sum_t - top_t - jnp.log(sum_t) + top_s + jnp.log(sum_s)
    weights = valid[:, 0].astype(jnp.float32)
    totals, numbers = lax.psum(
        (jnp.sum(divergence * weights, axis=(1, 2)), jnp.sum(weights, axis=(1, 2))), "space"
    )
    image_loss = totals / jnp.maximum(numbers, 1.0)
    return (divergence[:, None], image_loss)


def fits(rows):
    if rows % 32 or rows <= 128:
        return False
    first, second, far = middle(4 * rows)
    return second > first > 0 and first == far - second


def chosen(teacher_tokens, student_tokens, teacher_head, student_head, valid):
    operands = (teacher_tokens, student_tokens, teacher_head, student_head, valid)
    aligned = (
        lax.axis_size("space") == 4
        and lax.axis_size("mp") > 1
        and teacher_tokens.shape[2] % 16 == 0
        and teacher_tokens.shape[0] % 8 == 0
        and teacher_tokens.shape[0] * teacher_tokens.shape[2] % 128 == 0
        and all(fits(head.shape[0]) for head in (teacher_head, student_head))
    )
    return fused(*operands) if aligned else body(*operands)


def solution(mesh):
    in_specs = (
        P("dp", "space", None, None, None),
        P("dp", "space", None, None, None),
        P(("dp", "space"), "mp"),
        P(("dp", "space"), "mp"),
        P("dp", "space", None, None),
    )
    out_specs = (P("dp", "space", None, None), P("dp"))
    return jax.shard_map(chosen, mesh=mesh, in_specs=in_specs, out_specs=out_specs, check_vma=False)
```

time: 29.3 us -> 27 us (0.922)
  Pallas kernels: 28.5 us -> 26.2 us
    pallas_call x1, Pallas kernels: 27 us -> 25.5 us  [fused(): pl.pallas_call(functools.partial(kernel, edge, mp), out_shape=(pltpu.VMEM...]
    pallas_call x1, Pallas kernels: 1.48 us -> 0.65 us  [fused(): pl.pallas_call(finish, out_shape=(jax.ShapeDtypeStruct(kl.shape, F32), ja...]
where the time goes in v2:
time: 27 us; the launch traced here: 26.8 us
  Pallas kernels  26.2 us (97%)
  between operations  0.64 us (2%)
    pallas_call x1, Pallas kernels, fused(): pl.pallas_call(functools.partial(kernel, edge, mp), out_shape=(pltpu.VMEM...  25.5 us
    pallas_call x1, Pallas kernels, fused(): pl.pallas_call(finish, out_shape=(jax.ShapeDtypeStruct(kl.shape, F32), ja...  0.65 us

profile of v2, /device:TPU:0, one launch (start us, length us, event | category | flops | bytes accessed | tf_op | source)
XLA Modules:
  0.0 26.8 jit_solution(11880473588435675769)
XLA Ops:
  0.6 25.5 %shard_map.68 = (f32[8,16,16]{2,1,0:T(8,128)S(1)}, f32[1,8]{1,0:T(1,128)S(1)}) custom-call(bf16[8,256,1408]{2,1,0:T(8,128)(2,1)} %bitcast.7, bf16[8,256,1280]{2,1,0:T(8,128)(2,1)} %bitcast.8, bf16[352,250]{1,0:T(8,128)(2,1)} %wt_hbm.1, bf16[320,250]{1,0:T(8,128)(2,1)} %ws_hbm.1, s32[8,16,16]{2,1,0:T(8,128)} %bitcast.9), custom_call_target="tpu_custom_call" | custom-call | tf_op jit(solution)/shard_map/pallas_call | solution.py:394
  26.2 0.7 %shard_map.69 = (f32[8,16,16]{2,1,0:T(8,128)}, f32[1,8]{1,0:T(1,128)}) custom-call(f32[8,16,16]{2,1,0:T(8,128)S(1)} %get-tuple-element.6.kl_in, f32[1,8]{1,0:T(1,128)S(1)} %get-tuple-element.7.loss_in), custom_call_target="tpu_custom_call" | custom-call | tf_op jit(solution)/shard_map/pallas_call | solution.py:450

commit v3 on v2

--- a/solution.py
+++ b/solution.py
@@ -255,16 +255,15 @@
     turn(ws, ts_w, of_s.one_at, of_s.outer)
     turn(ws, ts_w, of_s.two_at, of_s.outer)
 
-    def student_outer(i, carry):
-        sl[i] += times(ts_w, ts.at[i], of_s.one_at, of_s.outer) + times(ts_w, ts.at[i], of_s.two_at, of_s.outer)
-        return carry
-
-    each(student_outer)
     arrive_far(1, ws, 1)
     turn(ws, ts_w, of_s.mid_at, of_s.inner)
 
     def student_stats(i, carry):
-        student = sl[i] + times(ts_w, ts.at[i], of_s.mid_at, of_s.inner)
+        student = sl[i] + (
+            times(ts_w, ts.at[i], of_s.one_at, of_s.outer)
+            + times(ts_w, ts.at[i], of_s.two_at, of_s.outer)
+            + times(ts_w, ts.at[i], of_s.mid_at, of_s.inner)
+        )
         sl[i] = student
         top = jnp.max(student, axis=0, keepdims=True)
         total = jnp.sum(jnp.exp(sl[i] - top), axis=0, keepdims=True)

time: 27 us -> 26.8 us (level)
  no operation moved by 1% of the time
where the time goes in v3:
time: 26.8 us; the launch traced here: 26.7 us
  Pallas kernels  26 us (97%)
  between operations  0.64 us (2%)
    pallas_call x1, Pallas kernels, fused(): pl.pallas_call(functools.partial(kernel, edge, mp), out_shape=(pltpu.VMEM...  25.4 us
    pallas_call x1, Pallas kernels, fused(): pl.pallas_call(finish, out_shape=(jax.ShapeDtypeStruct(kl.shape, F32), ja...  0.65 us

profile of v3, /device:TPU:0, one launch (start us, length us, event | category | flops | bytes accessed | tf_op | source)
XLA Modules:
  0.0 26.7 jit_solution(6462910958361806495)
XLA Ops:
  0.6 25.4 %shard_map.68 = (f32[8,16,16]{2,1,0:T(8,128)S(1)}, f32[1,8]{1,0:T(1,128)S(1)}) custom-call(bf16[8,256,1408]{2,1,0:T(8,128)(2,1)} %bitcast.7, bf16[8,256,1280]{2,1,0:T(8,128)(2,1)} %bitcast.8, bf16[352,250]{1,0:T(8,128)(2,1)} %wt_hbm.1, bf16[320,250]{1,0:T(8,128)(2,1)} %ws_hbm.1, s32[8,16,16]{2,1,0:T(8,128)} %bitcast.9), custom_call_target="tpu_custom_call" | custom-call | tf_op jit(solution)/shard_map/pallas_call | solution.py:393
  26.0 0.7 %shard_map.69 = (f32[8,16,16]{2,1,0:T(8,128)}, f32[1,8]{1,0:T(1,128)}) custom-call(f32[8,16,16]{2,1,0:T(8,128)S(1)} %get-tuple-element.6.kl_in, f32[1,8]{1,0:T(1,128)S(1)} %get-tuple-element.7.loss_in), custom_call_target="tpu_custom_call" | custom-call | tf_op jit(solution)/shard_map/pallas_call | solution.py:449
